TPU v7x, 32 devices: a whole 2x2x4 slice. The times are simulated.
32 devices in a mesh: grp: 2 (over y), node: 4 (over z), head: 4 (over x, core).
Axes of the slice: x: 2, y: 2, z: 4, core: 2. Of those that a mesh axis runs over, the one named last changes fastest.
Arguments:
- q_nope: bfloat16 [512, 8192], P(('grp', 'node'), 'head'), parts along dimension 0, may hold values from -400 to 400
- q_rope: bfloat16 [512, 4096], P(('grp', 'node'), 'head'), parts along dimension 0, may hold values from -6 to 6
- kv_new: bfloat16 [512, 576], P(('grp', 'node')), parts along dimension 0, may hold values from -6 to 6
- kv_gain: float32 [512], replicated, may hold values from 0.5 to 1.5
- cache: bfloat16 [192, 64, 576], P(('grp', 'node')), parts along dimension 0, may hold values from -6 to 6
- w_uk: bfloat16 [64, 128, 512], P('head', 'node'), may hold values from -0.5 to 0.5
- w_uv: bfloat16 [64, 512, 128], P('head', 'node'), may hold values from -1 to 1
- hit_pages: int32 [8, 4], P('grp'), parts along dimension 0, may hold values from 0 to 95, as said below
- hit_len: int32 [8], P('grp'), parts along dimension 0, may hold values from 1 to 256
- page_slots: int32 [8, 1], P('grp'), parts along dimension 0, may hold values from 0 to 95, as said below
Outputs:
- attn_out: bfloat16 [512, 8192], P(('grp', 'node'), 'head'), parts along dimension 0
- new_cache: bfloat16 [192, 64, 576], P(('grp', 'node')), parts along dimension 0
There are 2 independent parts, one for each index of `grp`. A program takes and returns all parts, laid end to end along the dimension named above; an argument that names none is the same for every part. Nothing has to cross between parts.
Inputs may be any that keep to these rules, and one draw needn't show every extreme that they name: `hit_pages`: page id = owner * 24 + local page; the owners named in one row are distinct. `page_slots`: page id = owner * 24 + local page; page p of session n lies with owner (n + p + 1) mod 4; no page is named twice.
All inputs are finite; a program needn't handle non-finite values.
Results may differ from a plain program's by a relative error of at most 0.012.
The roundings to bfloat16 on the way count: a program that leaves them out, or rounds other values in their place, can miss the bound.
Values may be sent and summed in bfloat16 or wider, within the bound.
A program may use at most 128 MiB of HBM per device.

v0:
```python
import functools
import math

import jax
import jax.numpy as jnp
from jax import lax
from jax.experimental import pallas as pl
from jax.experimental.pallas import tpu as pltpu
from jax.sharding import PartitionSpec as P

LATENT = 512
ROPE = 64
NOPE = 128
VHEAD = 128
BLOCK = 64
NEW = 64
BLK_DEV = 24
PHASES_K = 1
PHASES_V = 1
MESH = pl.DeviceIdType.MESH


def from_behind(block, axis, distance):
    devices = range(lax.axis_size(axis))
    route = [((i - distance) % len(devices), i) for i in devices]
    return lax.ppermute(block, axis, route)


def rotate(values, position):
    half_rope = ROPE // 2
    inverse = 10000.0 ** (-(jnp.arange(half_rope, dtype=jnp.float32) * 2.0 / ROPE))
    angles = position.astype(jnp.float32)[..., None] * inverse
    first_half = values[..., :half_rope]
    second_half = values[..., half_rope:]
    cosine = jnp.cos(angles)
    sine = jnp.sin(angles)
    return jnp.concatenate(
        [first_half * cosine - second_half * sine, first_half * sine + second_half * cosine],
        axis=-1,
    )


def make_pages(kv_rows, kv_gain, offset):
    latent = kv_rows[:, :LATENT].astype(jnp.float32)
    normed = latent * lax.rsqrt(jnp.mean(latent * latent, axis=-1, keepdims=True) + 1e-06) * kv_gain
    rotary = rotate(
        kv_rows[:, LATENT:].astype(jnp.float32),
        offset + jnp.arange(kv_rows.shape[0], dtype=jnp.int32),
    )
    return jnp.concatenate([normed, rotary], axis=-1).astype(jnp.bfloat16)


def select_rows(selector, blocks):
    flat = blocks.reshape(blocks.shape[0], -1)
    picked = jnp.dot(selector, flat, preferred_element_type=jnp.float32).astype(jnp.bfloat16)
    return picked.reshape((selector.shape[0],) + blocks.shape[1:])


def per_device(q_nope, q_rope, kv_new, kv_gain, cache, w_uk, w_uv, hit_pages, hit_len, page_slots):
    this_node = lax.axis_index("node")
    nodes = lax.axis_size("node")
    width = LATENT + ROPE
    heads_local = w_uk.shape[0]
    hits = hit_pages.shape[1]
    pages_each = NEW // BLOCK
    score_scale = 1.0 / math.sqrt(NOPE + ROPE)
    node_ids = jnp.arange(nodes, dtype=jnp.int32)
    new_index = jnp.arange(NEW, dtype=jnp.int32)
    offset = hit_len[this_node]
    new_pages = make_pages(kv_new, kv_gain, offset)
    page_blocks = new_pages.reshape(pages_each, BLOCK, width)
    own_pages = this_node * BLK_DEV + jnp.arange(BLK_DEV, dtype=jnp.int32)
    wanted = jnp.sum(
        (hit_pages[:, :, None] == own_pages[None, None, :]).astype(jnp.int32), axis=1
    ).astype(jnp.bfloat16)
    order_pick = ((hit_pages[this_node] // BLK_DEV)[:, None] == node_ids[None, :]).astype(
        jnp.bfloat16
    )
    columns = width // lax.axis_size("head")
    cache_part = lax.dynamic_slice_in_dim(cache, lax.axis_index("head") * columns, columns, 2)
    pulled = lax.all_to_all(
        select_rows(wanted, cache_part), "node", split_axis=0, concat_axis=0, tiled=True
    )
    prefix = select_rows(order_pick, pulled)
    prefix = lax.all_gather(prefix, "head", axis=2, tiled=True)
    q_rows = q_nope.reshape(NEW, heads_local, NOPE)
    q_pos = rotate(
        q_rope.reshape(NEW, heads_local, ROPE).astype(jnp.float32), (offset + new_index)[:, None]
    ).astype(jnp.bfloat16)
    q_pos = jnp.transpose(q_pos, (1, 0, 2))
    key_weight, value_weight = (
        lax.all_gather(w_uk, "node", axis=1, tiled=True),
        lax.all_gather(w_uv, "node", axis=1, tiled=True),
    )
    q_latent = jnp.einsum(
        "thk,hkc->htc", q_rows, key_weight, preferred_element_type=jnp.float32
    ).astype(jnp.bfloat16)
    key_rows = jnp.concatenate([prefix.reshape(hits * BLOCK, width), new_pages], axis=0)
    key_latent = key_rows[:, :LATENT]
    key_rotary = key_rows[:, LATENT:]
    prefix_seen = jnp.arange(hits * BLOCK, dtype=jnp.int32) < offset
    causal = new_index[None, :] <= new_index[:, None]
    visible = jnp.concatenate(
        [jnp.broadcast_to(prefix_seen[None, :], (NEW, hits * BLOCK)), causal], axis=1
    )
    target = max(1, 512 // NEW)
    group_size = 1
    for trial in range(1, heads_local + 1):
        if heads_local % trial == 0 and trial <= target:
            group_size = trial

    def attend(operands):
        q_part, r_part = operands
        scores = jnp.einsum("htc,kc->htk", q_part, key_latent, preferred_element_type=jnp.float32)
        scores = (
            scores
            + jnp.einsum("htr,kr->htk", r_part, key_rotary, preferred_element_type=jnp.float32)
        ) * score_scale
        scores = jnp.where(visible[None, :, :], scores, -1e30)
        row_max = jnp.max(scores, axis=-1, keepdims=True)
        expo_terms = jnp.where(visible[None, :, :], jnp.exp(scores - row_max), 0.0)
        weights = (expo_terms / jnp.sum(expo_terms, axis=-1, keepdims=True)).astype(jnp.bfloat16)
        return jnp.einsum(
            "htk,kc->htc", weights, key_latent, preferred_element_type=jnp.float32
        ).astype(jnp.bfloat16)

    groups = heads_local // group_size
    latent_out = lax.map(
        attend,
        (
            q_latent.reshape(groups, group_size, NEW, LATENT),
            q_pos.reshape(groups, group_size, NEW, ROPE),
        ),
    )
    latent_out = latent_out.reshape(heads_local, NEW, LATENT)
    projected = jnp.einsum(
        "htc,hcv->thv", latent_out, value_weight, preferred_element_type=jnp.float32
    )
    attn_out = projected.astype(jnp.bfloat16).reshape(NEW, heads_local * VHEAD)
    local_ids = jnp.arange(BLK_DEV, dtype=jnp.int32)
    new_cache = cache
    arrived = from_behind(page_blocks[0], "node", 1)
    sender = (this_node - 0 - 1 + nodes) % nodes
    slot = page_slots[sender, 0] - this_node * BLK_DEV
    new_cache = jnp.where((local_ids == slot)[:, None, None], arrived[None, :, :], new_cache)
    return (attn_out, new_cache)


def order(count):
    steps = []
    for near in range(1, count // 2 + 1):
        steps.append(near)
        if near != count - near:
            steps.append(count - near)
    return steps


def fused_kernel(
    nodes, grps, fan, phases_k, phases_v, score_scale,
    pages_ref, len_ref, slot_ref, freq_ref, gain_ref, qn_ref, qr_ref, kv_ref, cache_ref, uk_ref, uv_ref,
    attn_ref, out_ref,
    UK, UV, KB, CB, PAY, KV, Q, QR, QP, QL, LAT, OUT,
    zs_s, zs_r, f_s, f_r, q_s, q_r, k_s, k_r, wk_s, wk_r, yk_s, yk_r, wv_s, wv_r, yv_s, yv_r, loc, o_s, o_r,
):
    z = lax.axis_index("node")
    y = lax.axis_index("grp")
    hd = lax.axis_index("head")
    b = z % 2
    p = z // 2
    mate = z + 1 - 2 * b
    after = (z + 1) % nodes
    back = (z + nodes - 1) % nodes
    half = UK.shape[0]
    owned = cache_ref.shape[0]
    rows_k = uk_ref.shape[1]
    rows_v = uv_ref.shape[1]
    part = BLOCK // fan
    hits = pages_ref.shape[1]
    old = nodes * BLOCK
    steps = order(nodes)

    barrier = pltpu.get_barrier_semaphore()
    for k in range(1, nodes):
        pl.semaphore_signal(barrier, 1, device_id={"node": (z + k) % nodes}, device_id_type=MESH)
    for k in range(1, fan):
        pl.semaphore_signal(barrier, 1, device_id={"head": (hd + k) % fan}, device_id_type=MESH)
    pl.semaphore_signal(barrier, 1, device_id={"grp": 1 - y}, device_id_type=MESH)

    sends = []

    def remote(src, dst, send, recv, to):
        return pltpu.make_async_remote_copy(
            src_ref=src, dst_ref=dst, send_sem=send, recv_sem=recv, device_id=to, device_id_type=MESH
        )

    def go(*copy):
        copy = remote(*copy)
        copy.start()
        sends.append(copy)

    def arrive(block, send, recv, origin):
        remote(block, block, send, recv, origin).wait_recv()

    def key_part(node, head):
        at = pl.multiple_of(node * BLOCK + head * part, part)
        return KB.at[:, pl.ds(at, part), :]

    def kv_part(kind, head):
        return KV.at[kind, pl.ds(pl.multiple_of(head * part, part), part), :]

    mine = pl.ds(pl.multiple_of(b * NEW, NEW), NEW)
    theirs = pl.ds(pl.multiple_of((1 - b) * NEW, NEW), NEW)
    load = pltpu.make_async_copy(cache_ref, CB, loc.at[0])
    load.start()
    locals_ = [
        pltpu.make_async_copy(kv_ref, KV.at[2], loc.at[1]),
        pltpu.make_async_copy(uk_ref.at[pl.ds(b * half, half)], UK.at[:, pl.ds(pl.multiple_of(z * rows_k, rows_k), rows_k), :], loc.at[4]),
        pltpu.make_async_copy(uv_ref.at[pl.ds(b * half, half)], UV.at[:, pl.ds(pl.multiple_of(z * rows_v, rows_v), rows_v), :], loc.at[5]),
    ]
    for slot, (src, dst, wide) in enumerate(((qn_ref, Q, NOPE), (qr_ref, QR, ROPE))):
        cols = pl.ds(pl.multiple_of(b * half * wide, 128), half * wide)
        locals_.append(pltpu.make_async_copy(src.at[:, cols], dst.at[mine, :], loc.at[2 + slot]))
    for copy in locals_:
        copy.start()
    pl.semaphore_wait(barrier, nodes - 1 + fan - 1 + 1)

    kinds = (
        (uk_ref, UK, rows_k, phases_k, wk_s, wk_r, yk_s, yk_r),
        (uv_ref, UV, rows_v, phases_v, wv_s, wv_r, yv_s, yv_r),
    )

    def weight_part(kind, f, node, grp):
        buffer, rows, phases = kinds[kind][1:4]
        count = half // phases
        sub = count // grps
        return buffer.at[
            pl.ds(f * count + grp * sub, sub), pl.ds(pl.multiple_of(node * rows, rows), rows), :
        ]

    def send_weights(kind, f):
        src, _, _, phases, send, recv, _, _ = kinds[kind]
        count = half // phases
        sub = count // grps
        for k in steps:
            to = (z + k) % nodes
            rows = pl.ds((to % 2) * half + f * count + y * sub, sub)
            go(src.at[rows], weight_part(kind, f, z, y), send.at[f, k], recv.at[f, k], {"node": to})

    def pass_on(kind, f, which=steps):
        send, recv, over_s, over_r = kinds[kind][4:]
        for k in which:
            origin = (z + nodes - k) % nodes
            block = weight_part(kind, f, origin, y)
            arrive(block, send.at[f, k], recv.at[f, k], {"node": origin})
            go(block, block, over_s.at[f, k], over_r.at[f, k], {"grp": 1 - y})

    def take(kind, f):
        over_s, over_r = kinds[kind][6:]
        for k in steps:
            block = weight_part(kind, f, (z + nodes - k) % nodes, 1 - y)
            arrive(block, over_s.at[f, k], over_r.at[f, k], {"grp": 1 - y})

    quarter = pl.ds(pl.multiple_of(hd * part, part), part)
    send_weights(0, 0)
    for slot, (src, dst, wide) in enumerate(((qn_ref, Q, NOPE), (qr_ref, QR, ROPE))):
        cols = pl.ds(pl.multiple_of((1 - b) * half * wide, 128), half * wide)
        go(src.at[:, cols], dst.at[mine, :], q_s.at[slot], q_r.at[slot], {"node": mate})
    for kind, to in enumerate((mate, after)):
        go(kv_ref.at[quarter, :], kv_part(kind, hd), k_s.at[kind, 0], k_r.at[kind, 0], {"node": to})

    load.wait()

    def local_page(session):
        local = jnp.int32(0)
        for j in range(hits):
            page = pages_ref[session, j] - z * owned
            local = jnp.where((page >= 0) & (page < owned), page, local)
        return local

    for n in range(nodes):
        PAY[n] = CB[local_page(n), quarter, :]
    for i in range(2):
        KB[i, pl.ds(pl.multiple_of(z * BLOCK, BLOCK), BLOCK), :] = CB[local_page(2 * p + i)]

    def angles(session):
        at = (len_ref[session] + lax.broadcasted_iota(jnp.int32, (NEW, 128), 0)).astype(jnp.float32)
        turn = at * freq_ref[...]
        return jnp.cos(turn), jnp.sin(turn)

    turns = [angles(2 * p + i) for i in range(2)]
    turn_back = angles(back)
    for copy in locals_:
        copy.wait()

    def new_page(kind, cosine, sine):
        raw = KV[kind].astype(jnp.float32)
        latent = raw[:, :LATENT]
        mean = jnp.sum(latent * latent, axis=-1, keepdims=True) * (1.0 / LATENT)
        normed = latent * lax.rsqrt(mean + 1e-06) * gain_ref[...]
        rot = raw[:, LATENT:]
        swapped = jnp.concatenate([-rot[:, ROPE // 2:], rot[:, :ROPE // 2]], axis=-1)
        rotary = rot * cosine[:, :ROPE] + swapped * sine[:, :ROPE]
        return jnp.concatenate([normed, rotary], axis=-1).astype(jnp.bfloat16)

    KB[b, old:, :] = new_page(2, *[jnp.where(b == 0, t, u) for t, u in zip(*turns)])

    for k in steps:
        to = (z + k) % nodes
        go(
            PAY.at[pl.ds((to // 2) * 2, 2)], key_part(z, hd), zs_s.at[k], zs_r.at[k], {"node": to}
        )
    for f in range(1, phases_k):
        send_weights(0, f)
    for f in range(phases_v):
        send_weights(1, f)

    pass_on(0, 0)
    for slot, dst in enumerate((Q, QR)):
        arrive(dst.at[theirs, :], q_s.at[slot], q_r.at[slot], {"node": mate})
    for kind, origin in enumerate((mate, back)):
        block = kv_part(kind, hd)
        arrive(block, k_s.at[kind, 0], k_r.at[kind, 0], {"node": origin})
        for j in range(1, fan):
            go(block, block, k_s.at[kind, j], k_r.at[kind, j], {"head": (hd + j) % fan})
    for k in steps:
        origin = (z + nodes - k) % nodes
        block = key_part(origin, hd)
        arrive(block, zs_s.at[k], zs_r.at[k], {"node": origin})
        for j in range(1, fan):
            go(block, block, f_s.at[k, j], f_r.at[k, j], {"head": (hd + j) % fan})

    wide = half * ROPE
    first = (lax.broadcasted_iota(jnp.int32, (NEW, wide), 1) % ROPE) < ROPE // 2
    for i in range(2):
        cosine, sine = (jnp.concatenate([t] * (wide // 128), axis=1) for t in turns[i])
        x = QR[i * NEW:(i + 1) * NEW, :].astype(jnp.float32)
        ahead = pltpu.roll(x, wide - ROPE // 2, 1)
        behind = pltpu.roll(x, ROPE // 2, 1)
        turned = (x * cosine + jnp.where(first, -ahead, behind) * sine).astype(jnp.bfloat16)
        for h in range(half):
            QP[h, i * NEW:(i + 1) * NEW, :] = turned[:, h * ROPE:(h + 1) * ROPE]

    for kind in range(2):
        for j in range(1, fan):
            from_head = (hd + fan - j) % fan
            arrive(kv_part(kind, from_head), k_s.at[kind, j], k_r.at[kind, j], {"head": from_head})
    KB[1 - b, old:, :] = new_page(0, *[jnp.where(b == 0, u, t) for t, u in zip(*turns)])
    arrived = new_page(1, *turn_back)
    slot = slot_ref[back, 0] - z * owned

    def place(n, carry):
        CB[n] = jnp.where(slot == n, arrived, CB[n])
        return carry

    lax.fori_loop(0, owned, place, 0)

    for k in steps:
        origin = (z + nodes - k) % nodes
        for j in range(1, fan):
            from_head = (hd + fan - j) % fan
            arrive(key_part(origin, from_head), f_s.at[k, j], f_r.at[k, j], {"head": from_head})

    contract_last = (((1,), (1,)), ((), ()))
    total = old + NEW
    column = lax.broadcasted_iota(jnp.int32, (NEW, total), 1)
    token = lax.broadcasted_iota(jnp.int32, (NEW, total), 0)
    group = half // phases_k

    def attend(f, i):
        session = 2 * p + i
        seen = (column >= old) & (column - old <= token)
        for j in range(hits):
            local = column - (pages_ref[session, j] // owned) * BLOCK
            limit = jnp.minimum(len_ref[session] - j * BLOCK, BLOCK)
            seen = seen | ((column < old) & (local >= 0) & (local < limit))
        key_latent = KB[i, :, :LATENT]
        key_rotary = KB[i, :, LATENT:]
        heads = slice(f * group, (f + 1) * group)
        tokens = slice(i * NEW, (i + 1) * NEW)
        q_part = QL[heads, tokens, :].reshape(group * NEW, LATENT)
        r_part = QP[heads, tokens, :].reshape(group * NEW, ROPE)
        scores = lax.dot_general(q_part, key_latent, contract_last, preferred_element_type=jnp.float32)
        scores = scores + lax.dot_general(r_part, key_rotary, contract_last, preferred_element_type=jnp.float32)
        scores = (scores * score_scale).reshape(group, NEW, total)
        scores = jnp.where(seen[None], scores, -1e30)
        row_max = jnp.max(scores, axis=-1, keepdims=True)
        terms = jnp.where(seen[None], jnp.exp(scores - row_max), 0.0)
        weights = (terms / jnp.sum(terms, axis=-1, keepdims=True)).astype(jnp.bfloat16)
        mixed = jnp.dot(
            weights.reshape(group * NEW, total), key_latent, preferred_element_type=jnp.float32
        ).astype(jnp.bfloat16)
        LAT[heads, tokens, :] = mixed.reshape(group, NEW, LATENT)

    store = pltpu.make_async_copy(CB, out_ref, loc.at[0])
    for f in range(phases_k):
        if f > 0:
            pass_on(0, f)
        take(0, f)
        for h in range(f * group, (f + 1) * group):
            QL[h] = jnp.dot(
                Q[:, h * NOPE:(h + 1) * NOPE], UK[h], preferred_element_type=jnp.float32
            ).astype(jnp.bfloat16)
        attend(f, 0)
        if f == 0:
            store.start()
        if f == phases_k - 1:
            pass_on(1, 0, steps[:1])
        attend(f, 1)

    count = half // phases_v
    for f in range(phases_v):
        pass_on(1, f, steps if f > 0 else steps[1:])
        take(1, f)
        for h in range(f * count, (f + 1) * count):
            OUT[:, h * VHEAD:(h + 1) * VHEAD] = jnp.dot(
                LAT[h], UV[h], preferred_element_type=jnp.float32
            ).astype(jnp.bfloat16)
        here = pl.ds(f * count * VHEAD, count * VHEAD)
        there = pl.ds(pl.multiple_of((b * half + f * count) * VHEAD, 128), count * VHEAD)
        go(OUT.at[theirs, here], attn_ref.at[:, there], o_s.at[f], o_r.at[f], {"node": mate})
    cols = pl.ds(pl.multiple_of(b * half * VHEAD, 128), half * VHEAD)
    keep = pltpu.make_async_copy(OUT.at[mine, :], attn_ref.at[:, cols], loc.at[1])
    keep.start()
    for f in range(phases_v):
        there = pl.ds(pl.multiple_of(((1 - b) * half + f * count) * VHEAD, 128), count * VHEAD)
        block = attn_ref.at[:, there]
        arrive(block, o_s.at[f], o_r.at[f], {"node": mate})
    store.wait()
    keep.wait()
    for copy in sends:
        copy.wait_send()


def fused_device(q_nope, q_rope, kv_new, kv_gain, cache, w_uk, w_uv, hit_pages, hit_len, page_slots):
    nodes = lax.axis_size("node")
    grps = lax.axis_size("grp")
    fan = lax.axis_size("head")
    width = LATENT + ROPE
    owned = cache.shape[0]
    half = w_uk.shape[0] // 2
    phases_k = PHASES_K if half % (PHASES_K * grps) == 0 else 1
    phases_v = PHASES_V if half % (PHASES_V * grps) == 0 else 1
    vmem = pl.BlockSpec(memory_space=pltpu.VMEM)
    smem = pl.BlockSpec(memory_space=pltpu.SMEM)
    anywhere = pl.BlockSpec(memory_space=pl.ANY)
    bf16 = jnp.bfloat16
    inverse = 10000.0 ** (-(jnp.arange(ROPE // 2, dtype=jnp.float32) * 2.0 / ROPE))
    freq = jnp.tile(inverse, 128 // (ROPE // 2))[None, :]
    dma = pltpu.SemaphoreType.DMA
    k_sem = dma((phases_k, nodes))
    v_sem = dma((phases_v, nodes))
    return pl.pallas_call(
        functools.partial(
            fused_kernel, nodes, grps, fan, phases_k, phases_v, 1.0 / math.sqrt(NOPE + ROPE)
        ),
        name="fused",
        out_shape=(
            jax.ShapeDtypeStruct((NEW, 2 * half * VHEAD), bf16),
            jax.ShapeDtypeStruct(cache.shape, bf16),
        ),
        in_specs=[smem, smem, smem, vmem, vmem] + [anywhere] * 6,
        out_specs=(anywhere, anywhere),
        scratch_shapes=[
            pltpu.VMEM((half, NOPE, LATENT), bf16),
            pltpu.VMEM((half, LATENT, VHEAD), bf16),
            pltpu.VMEM((2, nodes * BLOCK + NEW, width), bf16),
            pltpu.VMEM(cache.shape, bf16),
            pltpu.VMEM((nodes, BLOCK // fan, width), bf16),
            pltpu.VMEM((3, NEW, width), bf16),
            pltpu.VMEM((2 * NEW, half * NOPE), bf16),
            pltpu.VMEM((2 * NEW, half * ROPE), bf16),
            pltpu.VMEM((half, 2 * NEW, ROPE), bf16),
            pltpu.VMEM((half, 2 * NEW, LATENT), bf16),
            pltpu.VMEM((half, 2 * NEW, LATENT), bf16),
            pltpu.VMEM((2 * NEW, half * VHEAD), bf16),
            dma((nodes,)), dma((nodes,)), dma((nodes, fan)), dma((nodes, fan)), dma((2,)), dma((2,)),
            dma((2, fan)), dma((2, fan)), k_sem, k_sem, k_sem, k_sem, v_sem, v_sem, v_sem, v_sem,
            dma((6,)), dma((phases_v,)), dma((phases_v,)),
        ],
        compiler_params=pltpu.CompilerParams(
            collective_id=0, has_side_effects=True, vmem_limit_bytes=60 << 20
        ),
    )(hit_pages, hit_len, page_slots, freq, kv_gain[None, :], q_nope, q_rope, kv_new, cache, w_uk, w_uv)


def choose(*operands):
    w_uk, w_uv = operands[5], operands[6]
    nodes, grps, fan = (lax.axis_size(name) for name in ("node", "grp", "head"))
    fits = (
        nodes % 2 == 0
        and grps == 2
        and NEW == BLOCK
        and BLOCK % (16 * fan) == 0
        and w_uk.shape[0] % 4 == 0
        and w_uk.shape[1] % 16 == 0
        and w_uv.shape[1] % 16 == 0
    )
    return (fused_device if fits else per_device)(*operands)


def solution(mesh):
    placed = (
        P(("grp", "node"), "head"),
        P(("grp", "node"), "head"),
        P(("grp", "node"), None),
        P(),
        P(("grp", "node"), None, None),
        P("head", "node", None),
        P("head", "node", None),
        P("grp", None),
        P("grp"),
        P("grp", None),
    )
    return jax.shard_map(
        choose,
        mesh=mesh,
        in_specs=placed,
        out_specs=(P(("grp", "node"), "head"), P(("grp", "node"), None, None)),
        check_vma=False,
    )
```

profile of v0, /device:TPU:0, one launch (start us, length us, event | category | flops | bytes accessed | tf_op | source)
XLA Modules:
  0.0 54.4 jit_solution(16097600484599458044)
XLA Ops:
  0.7 0.6 %broadcast_in_dim_tile.3.freq_ref = f32[1,128]{1,0:T(1,128)} reshape(f32[4,32]{1,0:T(4,128)S(1)} %tile.2) | data formatting | bytes 1024 | tf_op jit(solution)/shard_map/broadcast_in_dim;tile | solution.py:448
  1.2 1.3 %copy.12.slot_ref = s32[4,1]{1,0:T(4,128)} copy(s32[4,1]{0,1:T(1,128)} %param.19) | data formatting | bytes 32 | tf_op args[9]
  2.6 47.2 %fused.1 = (bf16[64,2048]{1,0:T(8,128)(2,1)}, bf16[24,64,576]{2,1,0:T(8,128)(2,1)}) custom-call(s32[4,4]{1,0:T(4,128)} %pages_ref.1, s32[4]{0:T(128)} %len_ref.1, s32[4,1]{1,0:T(4,128)} %copy.12.slot_ref, f32[1,128]{1,0:T(1,128)} %broadcast_in_dim_tile.3.freq_ref, f32[1,512]{1,0:T(1,128)} %bitcast.1, bf16[64,2048]{1,0:T(8,128)(2,1)} %qn_ref.1, ...), custom_call_target="tpu_custom_call" | custom-call | tf_op jit(solution)/shard_map/fused/pallas_call | solution.py:452
  49.8 1.7 %copy.15 = bf16[64,2048]{1,0:T(8,128)(2,1)} copy(bf16[64,2048]{1,0:T(8,128)(2,1)} %get-tuple-element.4) | data formatting | bytes 524288
  51.5 3.0 %copy.16 = bf16[24,64,576]{2,1,0:T(8,128)(2,1)} copy(bf16[24,64,576]{2,1,0:T(8,128)(2,1)} %get-tuple-element.5) | data formatting | bytes 3538944
  (2 shorter events, 0.0 us)
where the time goes:
time: 54.7 us; the launch traced here: 54.4 us
  Pallas kernels  47.2 us (86%)
  local copies, waits for them, and re-layouts  6.56 us (12%)
  between operations  0.65 us (1%)
    pallas_call x1, Pallas kernels, fused_device(): pl.pallas_call(functools.partial(fused_kernel, nodes, grps, fan, phases_k...  47.2 us
    unnamed x3, local copies, waits for them, and re-layouts  5.97 us

commit v1 on v0

--- a/solution.py
+++ b/solution.py
@@ -157,9 +157,9 @@
 
 def fused_kernel(
     nodes, grps, fan, phases_k, phases_v, score_scale,
-    pages_ref, len_ref, slot_ref, freq_ref, gain_ref, qn_ref, qr_ref, kv_ref, cache_ref, uk_ref, uv_ref,
-    attn_ref, out_ref,
-    UK, UV, KB, CB, PAY, KV, Q, QR, QP, QL, LAT, OUT,
+    pages_in, len_in, slot_in, gain_in, qn_ref, qr_ref, kv_ref, cache_ref, uk_ref, uv_ref,
+    attn_ref, CB,
+    UK, UV, KB, PAY, KV, Q, QR, QP, QL, LAT, OUT, pages_ref, len_ref, slot_ref, gain_ref,
     zs_s, zs_r, f_s, f_r, q_s, q_r, k_s, k_r, wk_s, wk_r, yk_s, yk_r, wv_s, wv_r, yv_s, yv_r, loc, o_s, o_r,
 ):
     z = lax.axis_index("node")
@@ -211,6 +211,14 @@
     mine = pl.ds(pl.multiple_of(b * NEW, NEW), NEW)
     theirs = pl.ds(pl.multiple_of((1 - b) * NEW, NEW), NEW)
     load = pltpu.make_async_copy(cache_ref, CB, loc.at[0])
+    tables = [
+        pltpu.make_async_copy(src, dst, loc.at[6 + i])
+        for i, (src, dst) in enumerate(
+            ((pages_in, pages_ref), (len_in, len_ref), (slot_in, slot_ref), (gain_in, gain_ref))
+        )
+    ]
+    for copy in tables:
+        copy.start()
     load.start()
     locals_ = [
         pltpu.make_async_copy(kv_ref, KV.at[2], loc.at[1]),
@@ -269,6 +277,8 @@
         go(kv_ref.at[quarter, :], kv_part(kind, hd), k_s.at[kind, 0], k_r.at[kind, 0], {"node": to})
 
     load.wait()
+    for copy in tables:
+        copy.wait()
 
     def local_page(session):
         local = jnp.int32(0)
@@ -282,9 +292,12 @@
     for i in range(2):
         KB[i, pl.ds(pl.multiple_of(z * BLOCK, BLOCK), BLOCK), :] = CB[local_page(2 * p + i)]
 
+    lane = lax.broadcasted_iota(jnp.int32, (1, 128), 1) % (ROPE // 2)
+    freq = jnp.exp(lane.astype(jnp.float32) * (-2.0 * math.log(10000.0) / ROPE))
+
     def angles(session):
         at = (len_ref[session] + lax.broadcasted_iota(jnp.int32, (NEW, 128), 0)).astype(jnp.float32)
-        turn = at * freq_ref[...]
+        turn = at * freq
         return jnp.cos(turn), jnp.sin(turn)
 
     turns = [angles(2 * p + i) for i in range(2)]
@@ -346,7 +359,7 @@
             arrive(kv_part(kind, from_head), k_s.at[kind, j], k_r.at[kind, j], {"head": from_head})
     KB[1 - b, old:, :] = new_page(0, *[jnp.where(b == 0, u, t) for t, u in zip(*turns)])
     arrived = new_page(1, *turn_back)
-    slot = slot_ref[back, 0] - z * owned
+    slot = slot_ref[0, back] - z * owned
 
     def place(n, carry):
         CB[n] = jnp.where(slot == n, arrived, CB[n])
@@ -391,7 +404,6 @@
         ).astype(jnp.bfloat16)
         LAT[heads, tokens, :] = mixed.reshape(group, NEW, LATENT)
 
-    store = pltpu.make_async_copy(CB, out_ref, loc.at[0])
     for f in range(phases_k):
         if f > 0:
             pass_on(0, f)
@@ -401,8 +413,6 @@
                 Q[:, h * NOPE:(h + 1) * NOPE], UK[h], preferred_element_type=jnp.float32
             ).astype(jnp.bfloat16)
         attend(f, 0)
-        if f == 0:
-            store.start()
         if f == phases_k - 1:
             pass_on(1, 0, steps[:1])
         attend(f, 1)
@@ -419,16 +429,24 @@
         there = pl.ds(pl.multiple_of((b * half + f * count) * VHEAD, 128), count * VHEAD)
         go(OUT.at[theirs, here], attn_ref.at[:, there], o_s.at[f], o_r.at[f], {"node": mate})
     cols = pl.ds(pl.multiple_of(b * half * VHEAD, 128), half * VHEAD)
-    keep = pltpu.make_async_copy(OUT.at[mine, :], attn_ref.at[:, cols], loc.at[1])
-    keep.start()
+    attn_ref[:, cols] = OUT[mine, :]
     for f in range(phases_v):
         there = pl.ds(pl.multiple_of(((1 - b) * half + f * count) * VHEAD, 128), count * VHEAD)
         block = attn_ref.at[:, there]
         arrive(block, o_s.at[f], o_r.at[f], {"node": mate})
-    store.wait()
-    keep.wait()
     for copy in sends:
         copy.wait_send()
+
+
+def write_kernel(attn_ref, pages_ref, attn_out, pages_out, done):
+    copies = [
+        pltpu.make_async_copy(attn_ref, attn_out, done.at[0]),
+        pltpu.make_async_copy(pages_ref, pages_out, done.at[1]),
+    ]
+    for copy in copies:
+        copy.start()
+    for copy in copies:
+        copy.wait()
 
 
 def fused_device(q_nope, q_rope, kv_new, kv_gain, cache, w_uk, w_uv, hit_pages, hit_len, page_slots):
@@ -441,30 +459,26 @@
     phases_k = PHASES_K if half % (PHASES_K * grps) == 0 else 1
     phases_v = PHASES_V if half % (PHASES_V * grps) == 0 else 1
     vmem = pl.BlockSpec(memory_space=pltpu.VMEM)
-    smem = pl.BlockSpec(memory_space=pltpu.SMEM)
     anywhere = pl.BlockSpec(memory_space=pl.ANY)
     bf16 = jnp.bfloat16
-    inverse = 10000.0 ** (-(jnp.arange(ROPE // 2, dtype=jnp.float32) * 2.0 / ROPE))
-    freq = jnp.tile(inverse, 128 // (ROPE // 2))[None, :]
     dma = pltpu.SemaphoreType.DMA
     k_sem = dma((phases_k, nodes))
     v_sem = dma((phases_v, nodes))
-    return pl.pallas_call(
+    attn, pages = pl.pallas_call(
         functools.partial(
             fused_kernel, nodes, grps, fan, phases_k, phases_v, 1.0 / math.sqrt(NOPE + ROPE)
         ),
         name="fused",
         out_shape=(
-            jax.ShapeDtypeStruct((NEW, 2 * half * VHEAD), bf16),
-            jax.ShapeDtypeStruct(cache.shape, bf16),
+            pltpu.VMEM((NEW, 2 * half * VHEAD), bf16),
+            pltpu.VMEM(cache.shape, bf16),
         ),
-        in_specs=[smem, smem, smem, vmem, vmem] + [anywhere] * 6,
-        out_specs=(anywhere, anywhere),
+        in_specs=[anywhere] * 10,
+        out_specs=(vmem, vmem),
         scratch_shapes=[
             pltpu.VMEM((half, NOPE, LATENT), bf16),
             pltpu.VMEM((half, LATENT, VHEAD), bf16),
             pltpu.VMEM((2, nodes * BLOCK + NEW, width), bf16),
-            pltpu.VMEM(cache.shape, bf16),
             pltpu.VMEM((nodes, BLOCK // fan, width), bf16),
             pltpu.VMEM((3, NEW, width), bf16),
             pltpu.VMEM((2 * NEW, half * NOPE), bf16),
@@ -473,14 +487,29 @@
             pltpu.VMEM((half, 2 * NEW, LATENT), bf16),
             pltpu.VMEM((half, 2 * NEW, LATENT), bf16),
             pltpu.VMEM((2 * NEW, half * VHEAD), bf16),
+            pltpu.SMEM(hit_pages.shape, jnp.int32),
+            pltpu.SMEM(hit_len.shape, jnp.int32),
+            pltpu.SMEM(page_slots.shape[::-1], jnp.int32),
+            pltpu.VMEM((1, LATENT), jnp.float32),
             dma((nodes,)), dma((nodes,)), dma((nodes, fan)), dma((nodes, fan)), dma((2,)), dma((2,)),
             dma((2, fan)), dma((2, fan)), k_sem, k_sem, k_sem, k_sem, v_sem, v_sem, v_sem, v_sem,
-            dma((6,)), dma((phases_v,)), dma((phases_v,)),
+            dma((10,)), dma((phases_v,)), dma((phases_v,)),
         ],
         compiler_params=pltpu.CompilerParams(
             collective_id=0, has_side_effects=True, vmem_limit_bytes=60 << 20
         ),
-    )(hit_pages, hit_len, page_slots, freq, kv_gain[None, :], q_nope, q_rope, kv_new, cache, w_uk, w_uv)
+    )(hit_pages, hit_len, page_slots.T, kv_gain[None, :], q_nope, q_rope, kv_new, cache, w_uk, w_uv)
+    return pl.pallas_call(
+        write_kernel,
+        name="write",
+        out_shape=(
+            jax.ShapeDtypeStruct(attn.shape, bf16),
+            jax.ShapeDtypeStruct(cache.shape, bf16),
+        ),
+        in_specs=[vmem, vmem],
+        out_specs=(anywhere, anywhere),
+        scratch_shapes=[dma((2,))],
+    )(*(pltpu.with_memory_space_constraint(x, pltpu.VMEM) for x in (attn, pages)))
 
 
 def choose(*operands):

time: 54.7 us -> 48.6 us (0.89)
  local copies, waits for them, and re-layouts: 6.56 us -> 0 us
  Pallas kernels: 47.2 us -> 47.8 us
    unnamed x3 -> x0, local copies, waits for them, and re-layouts: 5.97 us -> none
    pallas_call x0 -> x1, Pallas kernels: none -> 1.38 us  [fused_device(): pl.pallas_call(write_kernel, name='write', out_shape=(jax.ShapeDtypeStruc...]
    pallas_call x1, Pallas kernels: 47.2 us -> 46.4 us  [fused_device(): pl.pallas_call(functools.partial(fused_kernel, nodes, grps, fan, phases_k...]
    another operation x2 -> x0, local copies, waits for them, and re-layouts: 0.6 us -> none  [fused_device(): freq = jnp.tile(inverse, 128 // (ROPE // 2))[None, :]]
where the time goes in v1:
time: 48.6 us; the launch traced here: 48.4 us
  Pallas kernels  47.8 us (98%)
  between operations  0.64 us (1%)
    pallas_call x1, Pallas kernels, fused_device(): pl.pallas_call(functools.partial(fused_kernel, nodes, grps, fan, phases_k...  46.4 us
    pallas_call x1, Pallas kernels, fused_device(): pl.pallas_call(write_kernel, name='write', out_shape=(jax.ShapeDtypeStruc...  1.38 us

profile of v1, /device:TPU:0, one launch (start us, length us, event | category | flops | bytes accessed | tf_op | source)
XLA Modules:
  0.0 48.4 jit_solution(17365211714420953912)
XLA Ops:
  0.6 46.4 %fused.1 = (bf16[64,2048]{1,0:T(8,128)(2,1)S(1)}, bf16[24,64,576]{2,1,0:T(8,128)(2,1)S(1)}) custom-call(s32[4,4]{1,0:T(4,128)} %pages_in.1, s32[4]{0:T(128)} %len_in.1, s32[1,4]{1,0:T(1,128)} %bitcast.3, f32[1,512]{1,0:T(1,128)} %bitcast.2, bf16[64,2048]{1,0:T(8,128)(2,1)} %qn_ref.1, bf16[64,1024]{1,0:T(8,128)(2,1)} %qr_ref.1, bf16[64,576]{1,0:T(8,128)(2,1)} %kv_ref.1, ...), custom_call_target="tpu_custom_call" | custom-call | tf_op jit(solution)/shard_map/fused/pallas_call | solution.py:467
  47.1 1.4 %write.1 = (bf16[64,2048]{1,0:T(8,128)(2,1)}, bf16[24,64,576]{2,1,0:T(8,128)(2,1)}) custom-call(bf16[64,2048]{1,0:T(8,128)(2,1)S(1)} %get-tuple-element.4.attn_ref, bf16[24,64,576]{2,1,0:T(8,128)(2,1)S(1)} %get-tuple-element.5.pages_ref), custom_call_target="tpu_custom_call" | custom-call | tf_op jit(solution)/shard_map/write/pallas_call | solution.py:502

commit v2 on v1

v2 whole, which is shorter than its diff:
```python
import functools
import math

import jax
import jax.numpy as jnp
from jax import lax
from jax.experimental import pallas as pl
from jax.experimental.pallas import tpu as pltpu
from jax.sharding import PartitionSpec as P

LATENT = 512
ROPE = 64
NOPE = 128
VHEAD = 128
BLOCK = 64
NEW = 64
BLK_DEV = 24
PHASES = 4
MESH = pl.DeviceIdType.MESH


def from_behind(block, axis, distance):
    devices = range(lax.axis_size(axis))
    route = [((i - distance) % len(devices), i) for i in devices]
    return lax.ppermute(block, axis, route)


def rotate(values, position):
    half_rope = ROPE // 2
    inverse = 10000.0 ** (-(jnp.arange(half_rope, dtype=jnp.float32) * 2.0 / ROPE))
    angles = position.astype(jnp.float32)[..., None] * inverse
    first_half = values[..., :half_rope]
    second_half = values[..., half_rope:]
    cosine = jnp.cos(angles)
    sine = jnp.sin(angles)
    return jnp.concatenate(
        [first_half * cosine - second_half * sine, first_half * sine + second_half * cosine],
        axis=-1,
    )


def make_pages(kv_rows, kv_gain, offset):
    latent = kv_rows[:, :LATENT].astype(jnp.float32)
    normed = latent * lax.rsqrt(jnp.mean(latent * latent, axis=-1, keepdims=True) + 1e-06) * kv_gain
    rotary = rotate(
        kv_rows[:, LATENT:].astype(jnp.float32),
        offset + jnp.arange(kv_rows.shape[0], dtype=jnp.int32),
    )
    return jnp.concatenate([normed, rotary], axis=-1).astype(jnp.bfloat16)


def select_rows(selector, blocks):
    flat = blocks.reshape(blocks.shape[0], -1)
    picked = jnp.dot(selector, flat, preferred_element_type=jnp.float32).astype(jnp.bfloat16)
    return picked.reshape((selector.shape[0],) + blocks.shape[1:])


def per_device(q_nope, q_rope, kv_new, kv_gain, cache, w_uk, w_uv, hit_pages, hit_len, page_slots):
    this_node = lax.axis_index("node")
    nodes = lax.axis_size("node")
    width = LATENT + ROPE
    heads_local = w_uk.shape[0]
    hits = hit_pages.shape[1]
    pages_each = NEW // BLOCK
    score_scale = 1.0 / math.sqrt(NOPE + ROPE)
    node_ids = jnp.arange(nodes, dtype=jnp.int32)
    new_index = jnp.arange(NEW, dtype=jnp.int32)
    offset = hit_len[this_node]
    new_pages = make_pages(kv_new, kv_gain, offset)
    page_blocks = new_pages.reshape(pages_each, BLOCK, width)
    own_pages = this_node * BLK_DEV + jnp.arange(BLK_DEV, dtype=jnp.int32)
    wanted = jnp.sum(
        (hit_pages[:, :, None] == own_pages[None, None, :]).astype(jnp.int32), axis=1
    ).astype(jnp.bfloat16)
    order_pick = ((hit_pages[this_node] // BLK_DEV)[:, None] == node_ids[None, :]).astype(
        jnp.bfloat16
    )
    columns = width // lax.axis_size("head")
    cache_part = lax.dynamic_slice_in_dim(cache, lax.axis_index("head") * columns, columns, 2)
    pulled = lax.all_to_all(
        select_rows(wanted, cache_part), "node", split_axis=0, concat_axis=0, tiled=True
    )
    prefix = select_rows(order_pick, pulled)
    prefix = lax.all_gather(prefix, "head", axis=2, tiled=True)
    q_rows = q_nope.reshape(NEW, heads_local, NOPE)
    q_pos = rotate(
        q_rope.reshape(NEW, heads_local, ROPE).astype(jnp.float32), (offset + new_index)[:, None]
    ).astype(jnp.bfloat16)
    q_pos = jnp.transpose(q_pos, (1, 0, 2))
    key_weight, value_weight = (
        lax.all_gather(w_uk, "node", axis=1, tiled=True),
        lax.all_gather(w_uv, "node", axis=1, tiled=True),
    )
    q_latent = jnp.einsum(
        "thk,hkc->htc", q_rows, key_weight, preferred_element_type=jnp.float32
    ).astype(jnp.bfloat16)
    key_rows = jnp.concatenate([prefix.reshape(hits * BLOCK, width), new_pages], axis=0)
    key_latent = key_rows[:, :LATENT]
    key_rotary = key_rows[:, LATENT:]
    prefix_seen = jnp.arange(hits * BLOCK, dtype=jnp.int32) < offset
    causal = new_index[None, :] <= new_index[:, None]
    visible = jnp.concatenate(
        [jnp.broadcast_to(prefix_seen[None, :], (NEW, hits * BLOCK)), causal], axis=1
    )
    target = max(1, 512 // NEW)
    group_size = 1
    for trial in range(1, heads_local + 1):
        if heads_local % trial == 0 and trial <= target:
            group_size = trial

    def attend(operands):
        q_part, r_part = operands
        scores = jnp.einsum("htc,kc->htk", q_part, key_latent, preferred_element_type=jnp.float32)
        scores = (
            scores
            + jnp.einsum("htr,kr->htk", r_part, key_rotary, preferred_element_type=jnp.float32)
        ) * score_scale
        scores = jnp.where(visible[None, :, :], scores, -1e30)
        row_max = jnp.max(scores, axis=-1, keepdims=True)
        expo_terms = jnp.where(visible[None, :, :], jnp.exp(scores - row_max), 0.0)
        weights = (expo_terms / jnp.sum(expo_terms, axis=-1, keepdims=True)).astype(jnp.bfloat16)
        return jnp.einsum(
            "htk,kc->htc", weights, key_latent, preferred_element_type=jnp.float32
        ).astype(jnp.bfloat16)

    groups = heads_local // group_size
    latent_out = lax.map(
        attend,
        (
            q_latent.reshape(groups, group_size, NEW, LATENT),
            q_pos.reshape(groups, group_size, NEW, ROPE),
        ),
    )
    latent_out = latent_out.reshape(heads_local, NEW, LATENT)
    projected = jnp.einsum(
        "htc,hcv->thv", latent_out, value_weight, preferred_element_type=jnp.float32
    )
    attn_out = projected.astype(jnp.bfloat16).reshape(NEW, heads_local * VHEAD)
    local_ids = jnp.arange(BLK_DEV, dtype=jnp.int32)
    new_cache = cache
    arrived = from_behind(page_blocks[0], "node", 1)
    sender = (this_node - 0 - 1 + nodes) % nodes
    slot = page_slots[sender, 0] - this_node * BLK_DEV
    new_cache = jnp.where((local_ids == slot)[:, None, None], arrived[None, :, :], new_cache)
    return (attn_out, new_cache)


def fused_kernel(
    nodes, phases, score_scale,
    pages_in, len_in, slot_in, gain_in, qn_ref, qr_ref, kv_ref, cache_ref, uk_ref, uv_ref,
    attn_ref, CB,
    UK, UV, KB, PAY, KV, Q, QR, QT, QP, QL, LAT, OUT, SEEN, pages_ref, len_ref, slot_ref, gain_ref,
    loc, e_s, e_r, c_s, c_r, n_s, n_r, q_s, q_r, t_s, t_r, m_s, m_r,
    x_s, x_r, d_s, d_r, g_s, g_r, wk_s, wk_r, wv_s, wv_r, o_s, o_r,
):
    z = lax.axis_index("node")
    y = lax.axis_index("grp")
    hd = lax.axis_index("head")
    b = z % 2
    p = z // 2
    me = 2 * y + b
    mate = z + 1 - 2 * b
    after = (z + 1) % nodes
    back = (z + nodes - 1) % nodes
    heads = UK.shape[0]
    owned = cache_ref.shape[0]
    rows_k = uk_ref.shape[1]
    rows_v = uv_ref.shape[1]
    part = BLOCK // 4
    hits = pages_ref.shape[1]
    old = nodes * BLOCK
    total = old + NEW
    near = hd + 1 - 2 * (hd % 2)
    across = (hd + 2) % 4
    team = (
        (2 * y + 1 - b, {"node": mate}),
        (2 * (1 - y) + b, {"grp": 1 - y}),
        (2 * (1 - y) + 1 - b, {"grp": 1 - y, "node": mate}),
    )
    peers = [mate]
    for j in range(1, nodes // 2):
        q = (p + j) % (nodes // 2)
        inner = jnp.where(q < p, 1, 0)
        peers = peers + [2 * q + inner, 2 * q + 1 - inner]
    outward = peers[::-1]

    def way(to):
        return (to - z + nodes) % nodes

    def road(origin):
        return (z - origin + nodes) % nodes


    barrier = pltpu.get_barrier_semaphore()
    for k in range(1, nodes):
        pl.semaphore_signal(barrier, 1, device_id={"node": (z + k) % nodes}, device_id_type=MESH)
    for to in (team[1][1], team[2][1], {"head": near}, {"head": across}):
        pl.semaphore_signal(barrier, 1, device_id=to, device_id_type=MESH)

    sends = []

    def remote(src, dst, send, recv, to):
        return pltpu.make_async_remote_copy(
            src_ref=src, dst_ref=dst, send_sem=send, recv_sem=recv, device_id=to, device_id_type=MESH
        )

    def go(*copy):
        copy = remote(*copy)
        copy.start()
        sends.append(copy)

    def arrive(block, send, recv, origin):
        remote(block, block, send, recv, origin).wait_recv()

    def rows_of(head):
        return pl.ds(pl.multiple_of(head * part, part), part)

    def cols_of(who, wide):
        return pl.ds(pl.multiple_of(who * heads * wide, 128), heads * wide)

    quarter = rows_of(hd)
    ours = pl.ds(2 * y, 2)

    def local(src, dst, slot):
        copy = pltpu.make_async_copy(src, dst, loc.at[slot])
        copy.start()
        return copy

    def mine(who):
        return pl.ds(who * heads, heads)

    early = [
        local(pages_in, pages_ref, 0),
        local(len_in, len_ref, 1),
        local(slot_in, slot_ref, 2),
        local(gain_in, gain_ref, 3),
        local(kv_ref.at[quarter, :], KV, 4),
        local(qr_ref, QR, 5),
    ]
    load = local(cache_ref, CB, 6)
    late = [
        local(qn_ref.at[:, cols_of(me, NOPE)], Q.at[me], 7),
        local(uk_ref.at[mine(me)], UK.at[:, pl.ds(pl.multiple_of(z * rows_k, rows_k), rows_k), :], 8),
        local(uv_ref.at[mine(me)], UV.at[:, pl.ds(pl.multiple_of(z * rows_v, rows_v), rows_v), :], 9),
    ]
    def weight_part(buffer, rows, first, count, node):
        return buffer.at[pl.ds(first, count), pl.ds(pl.multiple_of(node * rows, rows), rows), :]

    splits = ((0, 1), (1, heads - 1))

    def send_keys(c, to):
        first, some = splits[c]
        src = uk_ref.at[pl.ds((2 * y + to % 2) * heads + first, some)]
        k = way(to)
        go(src, weight_part(UK, rows_k, first, some, z), wk_s.at[c, k], wk_r.at[c, k], {"node": to})

    pl.semaphore_wait(barrier, nodes - 1 + 4)
    send_keys(0, outward[0])
    for copy in early:
        copy.wait()

    lane = lax.broadcasted_iota(jnp.int32, (1, 128), 1) % (ROPE // 2)
    freq = jnp.exp(lane.astype(jnp.float32) * (-2.0 * math.log(10000.0) / ROPE))

    def angles(first, count):
        at = (first + lax.broadcasted_iota(jnp.int32, (count, 128), 0)).astype(jnp.float32)
        turn = at * freq
        return jnp.cos(turn), jnp.sin(turn)

    raw = KV[...].astype(jnp.float32)
    latent = raw[:, :LATENT]
    mean = jnp.sum(latent * latent, axis=-1, keepdims=True) * (1.0 / LATENT)
    normed = latent * lax.rsqrt(mean + 1e-06) * gain_ref[...]
    rot = raw[:, LATENT:]
    swapped = jnp.concatenate([-rot[:, ROPE // 2:], rot[:, :ROPE // 2]], axis=-1)
    cosine, sine = angles(len_ref[z] + hd * part, part)
    rotary = rot * cosine[:, :ROPE] + swapped * sine[:, :ROPE]
    KB[me, nodes, quarter, :] = jnp.concatenate([normed, rotary], axis=-1).astype(jnp.bfloat16)

    column = lax.broadcasted_iota(jnp.int32, (8, old), 1)
    for i in range(2):
        session = 2 * p + i
        seen = column < 0
        for j in range(hits):
            place = column - (pages_ref[session, j] // owned) * BLOCK
            limit = jnp.minimum(len_ref[session] - j * BLOCK, BLOCK)
            seen = seen | ((place >= 0) & (place < limit))
        SEEN[2 * y + i] = jnp.where(seen, 1.0, 0.0)

    wide = 4 * heads * ROPE
    first = (lax.broadcasted_iota(jnp.int32, (NEW, wide), 1) % ROPE) < ROPE // 2
    cosine, sine = (jnp.concatenate([t] * (wide // 128), axis=1) for t in angles(len_ref[z], NEW))
    x = QR[...].astype(jnp.float32)
    ahead = pltpu.roll(x, wide - ROPE // 2, 1)
    behind = pltpu.roll(x, ROPE // 2, 1)
    QT[...] = (x * cosine + jnp.where(first, -ahead, behind) * sine).astype(jnp.bfloat16)

    load.wait()

    def local_page(session):
        found = jnp.int32(0)
        for j in range(hits):
            page = pages_ref[session, j] - z * owned
            found = jnp.where((page >= 0) & (page < owned), page, found)
        return found

    for n in range(nodes):
        PAY[n] = CB[local_page(n), quarter, :]
    for i in range(2):
        KB[2 * y + i, z, quarter, :] = CB[local_page(2 * p + i), quarter, :]

    def pages_at(group, owner):
        return KB.at[pl.ds(2 * group, 2), owner, quarter, :]

    def new_at(who):
        return KB.at[who, nodes, quarter, :]

    count = heads // phases

    def spread_part(group, origin, head):
        return KB.at[pl.ds(2 * group, 2), origin, rows_of(head), :]

    def fresh_part(head):
        return KB.at[:, nodes, rows_of(head), :]

    def spread(block, m):
        go(block, block, x_s.at[m], x_r.at[m], {"head": across})
        go(block, block, d_s.at[m], d_r.at[m], {"head": near})

    def relay(block, m):
        arrive(block, x_s.at[m], x_r.at[m], {"head": across})
        go(block, block, g_s.at[m], g_r.at[m], {"head": near})

    for to in outward:
        k = way(to)
        go(PAY.at[pl.ds((to // 2) * 2, 2)], pages_at(y, z), e_s.at[k], e_r.at[k], {"node": to})
    go(pages_at(y, z), pages_at(y, z), c_s.at[0], c_r.at[0], {"grp": 1 - y})
    spread(pages_at(y, z), 0)
    for d, (who, to) in enumerate(team):
        go(new_at(me), new_at(me), n_s.at[d], n_r.at[d], to)
    go(new_at(me), new_at(4), n_s.at[3], n_r.at[3], {"node": after})
    go(SEEN.at[ours], SEEN.at[ours], m_s.at[0], m_r.at[0], {"grp": 1 - y})
    send_keys(1, outward[0])
    for to in outward[1:]:
        send_keys(0, to)
        send_keys(1, to)

    def send_queries(d):
        who, to = team[d]
        go(QT.at[:, cols_of(who, ROPE)], QP.at[me], t_s.at[d], t_r.at[d], to)
        go(qn_ref.at[:, cols_of(who, NOPE)], Q.at[me], q_s.at[d], q_r.at[d], to)

    send_queries(0)
    QP[me] = QT[:, cols_of(me, ROPE)]
    for origin in peers:
        k = road(origin)
        block = pages_at(y, origin)
        arrive(block, e_s.at[k], e_r.at[k], {"node": origin})
        go(block, block, c_s.at[k], c_r.at[k], {"grp": 1 - y})
        spread(block, k)
    send_queries(2)
    send_queries(1)
    for f in range(phases):
        for to in outward:
            k = way(to)
            src = uv_ref.at[pl.ds((2 * y + to % 2) * heads + f * count, count)]
            go(src, weight_part(UV, rows_v, f * count, count, z), wv_s.at[f, k], wv_r.at[f, k], {"node": to})
    for origin in [z] + peers:
        k = road(origin)
        block = pages_at(1 - y, origin)
        arrive(block, c_s.at[k], c_r.at[k], {"grp": 1 - y})
        spread(block, nodes + k)
    for d, (who, to) in enumerate(team):
        arrive(new_at(who), n_s.at[d], n_r.at[d], to)
    arrive(new_at(4), n_s.at[3], n_r.at[3], {"node": back})
    spread(fresh_part(hd), 2 * nodes)
    far = near + 2 - 4 * (near // 2)
    for group in range(2):
        for origin in [z] + peers:
            relay(spread_part(y if group == 0 else 1 - y, origin, across), group * nodes + road(origin))
    relay(fresh_part(across), 2 * nodes)
    for head, r in ((near, d_r), (far, g_r)):
        for group in range(2):
            for origin in [z] + peers:
                m = group * nodes + road(origin)
                arrive(spread_part(y if group == 0 else 1 - y, origin, head), d_s.at[m], r.at[m], {"head": near})
        arrive(fresh_part(head), d_s.at[2 * nodes], r.at[2 * nodes], {"head": near})

    arrived = KB[4, nodes]
    slot = slot_ref[0, back] - z * owned

    def place(n, carry):
        CB[n] = jnp.where(slot == n, arrived, CB[n])
        return carry

    lax.fori_loop(0, owned, place, 0)

    arrive(SEEN.at[pl.ds(2 * (1 - y), 2)], m_s.at[0], m_r.at[0], {"grp": 1 - y})
    for copy in late:
        copy.wait()
    for d, (who, to) in enumerate(team):
        arrive(QP.at[who], t_s.at[d], t_r.at[d], to)
        arrive(Q.at[who], q_s.at[d], q_r.at[d], to)
    for origin in peers:
        k = road(origin)
        for c, (first_head, some) in enumerate(splits):
            block = weight_part(UK, rows_k, first_head, some, origin)
            arrive(block, wk_s.at[c, k], wk_r.at[c, k], {"node": origin})

    for h in range(heads):
        QL[h] = jnp.dot(
            Q[:, :, h * NOPE:(h + 1) * NOPE].reshape(4 * NEW, NOPE), UK[h], preferred_element_type=jnp.float32
        ).astype(jnp.bfloat16)

    contract_last = (((1,), (1,)), ((), ()))
    causal = lax.broadcasted_iota(jnp.int32, (NEW, NEW), 1) <= lax.broadcasted_iota(jnp.int32, (NEW, NEW), 0)
    causal = jnp.where(causal, 1.0, 0.0)
    for i in range(4):
        seen = jnp.concatenate([jnp.broadcast_to(SEEN[i, 0:1, :], (NEW, old)), causal], axis=1) > 0.5
        keys = KB[i].reshape(total, LATENT + ROPE)
        key_latent = keys[:, :LATENT]
        tokens = slice(i * NEW, (i + 1) * NEW)
        q_part = QL[:, tokens, :].reshape(heads * NEW, LATENT)
        r_part = jnp.concatenate([QP[i, :, h * ROPE:(h + 1) * ROPE] for h in range(heads)], axis=0)
        scores = lax.dot_general(q_part, key_latent, contract_last, preferred_element_type=jnp.float32)
        scores = scores + lax.dot_general(r_part, keys[:, LATENT:], contract_last, preferred_element_type=jnp.float32)
        scores = (scores * score_scale).reshape(heads, NEW, total)
        scores = jnp.where(seen[None], scores, -1e30)
        row_max = jnp.max(scores, axis=-1, keepdims=True)
        terms = jnp.where(seen[None], jnp.exp(scores - row_max), 0.0)
        weights = (terms / jnp.sum(terms, axis=-1, keepdims=True)).astype(jnp.bfloat16)
        mixed = jnp.dot(
            weights.reshape(heads * NEW, total), key_latent, preferred_element_type=jnp.float32
        ).astype(jnp.bfloat16)
        LAT[:, tokens, :] = mixed.reshape(heads, NEW, LATENT)

    def result_part(who, f):
        return attn_ref.at[:, pl.ds(pl.multiple_of((who * heads + f * count) * VHEAD, 128), count * VHEAD)]

    for f in range(phases):
        for origin in peers:
            k = road(origin)
            block = weight_part(UV, rows_v, f * count, count, origin)
            arrive(block, wv_s.at[f, k], wv_r.at[f, k], {"node": origin})
        for h in range(f * count, (f + 1) * count):
            OUT[:, :, h * VHEAD:(h + 1) * VHEAD] = jnp.dot(
                LAT[h], UV[h], preferred_element_type=jnp.float32
            ).astype(jnp.bfloat16).reshape(4, NEW, VHEAD)
        here = pl.ds(f * count * VHEAD, count * VHEAD)
        for d in (2, 0, 1):
            who, to = team[d]
            go(OUT.at[who, :, here], result_part(me, f), o_s.at[f, d], o_r.at[f, d], to)
    attn_ref[:, cols_of(me, VHEAD)] = OUT[me]
    for f in range(phases):
        for d, (who, to) in enumerate(team):
            arrive(result_part(who, f), o_s.at[f, d], o_r.at[f, d], to)
    for copy in sends:
        copy.wait_send()


def write_kernel(attn_ref, pages_ref, attn_out, pages_out, done):
    copies = [
        pltpu.make_async_copy(attn_ref, attn_out, done.at[0]),
        pltpu.make_async_copy(pages_ref, pages_out, done.at[1]),
    ]
    for copy in copies:
        copy.start()
    for copy in copies:
        copy.wait()


def fused_device(q_nope, q_rope, kv_new, kv_gain, cache, w_uk, w_uv, hit_pages, hit_len, page_slots):
    nodes = lax.axis_size("node")
    width = LATENT + ROPE
    heads = w_uk.shape[0] // 4
    phases = PHASES if heads % PHASES == 0 else 1
    vmem = pl.BlockSpec(memory_space=pltpu.VMEM)
    anywhere = pl.BlockSpec(memory_space=pl.ANY)
    bf16 = jnp.bfloat16
    dma = pltpu.SemaphoreType.DMA

    def pair(*shape):
        return [dma(shape), dma(shape)]

    attn, pages = pl.pallas_call(
        functools.partial(fused_kernel, nodes, phases, 1.0 / math.sqrt(NOPE + ROPE)),
        name="fused",
        out_shape=(
            pltpu.VMEM((NEW, 4 * heads * VHEAD), bf16),
            pltpu.VMEM(cache.shape, bf16),
        ),
        in_specs=[anywhere] * 10,
        out_specs=(vmem, vmem),
        scratch_shapes=[
            pltpu.VMEM((heads, NOPE, LATENT), bf16),
            pltpu.VMEM((heads, LATENT, VHEAD), bf16),
            pltpu.VMEM((5, nodes + 1, BLOCK, width), bf16),
            pltpu.VMEM((nodes, BLOCK // 4, width), bf16),
            pltpu.VMEM((BLOCK // 4, width), bf16),
            pltpu.VMEM((4, NEW, heads * NOPE), bf16),
            pltpu.VMEM((NEW, 4 * heads * ROPE), bf16),
            pltpu.VMEM((NEW, 4 * heads * ROPE), bf16),
            pltpu.VMEM((4, NEW, heads * ROPE), bf16),
            pltpu.VMEM((heads, 4 * NEW, LATENT), bf16),
            pltpu.VMEM((heads, 4 * NEW, LATENT), bf16),
            pltpu.VMEM((4, NEW, heads * VHEAD), bf16),
            pltpu.VMEM((4, 8, nodes * BLOCK), jnp.float32),
            pltpu.SMEM(hit_pages.shape, jnp.int32),
            pltpu.SMEM(hit_len.shape, jnp.int32),
            pltpu.SMEM(page_slots.shape[::-1], jnp.int32),
            pltpu.VMEM((1, LATENT), jnp.float32),
            dma((10,)),
            *pair(nodes), *pair(nodes), *pair(4), *pair(3), *pair(3), *pair(1),
            *pair(2 * nodes + 1), *pair(2 * nodes + 1), *pair(2 * nodes + 1), *pair(2, nodes), *pair(phases, nodes), *pair(phases, 3),
        ],
        compiler_params=pltpu.CompilerParams(
            collective_id=0, has_side_effects=True, vmem_limit_bytes=60 << 20
        ),
    )(hit_pages, hit_len, page_slots.T, kv_gain[None, :], q_nope, q_rope, kv_new, cache, w_uk, w_uv)
    return pl.pallas_call(
        write_kernel,
        name="write",
        out_shape=(
            jax.ShapeDtypeStruct(attn.shape, bf16),
            jax.ShapeDtypeStruct(cache.shape, bf16),
        ),
        in_specs=[vmem, vmem],
        out_specs=(anywhere, anywhere),
        scratch_shapes=[dma((2,))],
    )(*(pltpu.with_memory_space_constraint(x, pltpu.VMEM) for x in (attn, pages)))


def choose(*operands):
    w_uk, w_uv = operands[5], operands[6]
    nodes, grps, fan = (lax.axis_size(name) for name in ("node", "grp", "head"))
    fits = (
        nodes % 2 == 0
        and grps == 2
        and fan == 4
        and NEW == BLOCK
        and w_uk.shape[0] % 8 == 0
        and w_uk.shape[1] % 16 == 0
        and w_uv.shape[1] % 16 == 0
    )
    return (fused_device if fits else per_device)(*operands)


def solution(mesh):
    placed = (
        P(("grp", "node"), "head"),
        P(("grp", "node"), "head"),
        P(("grp", "node"), None),
        P(),
        P(("grp", "node"), None, None),
        P("head", "node", None),
        P("head", "node", None),
        P("grp", None),
        P("grp"),
        P("grp", None),
    )
    return jax.shard_map(
        choose,
        mesh=mesh,
        in_specs=placed,
        out_specs=(P(("grp", "node"), "head"), P(("grp", "node"), None, None)),
        check_vma=False,
    )
```

time: 48.6 us -> 40.8 us (0.84)
  Pallas kernels: 47.8 us -> 40 us
    pallas_call x1, Pallas kernels: 46.4 us -> 38.6 us  [fused_device(): pl.pallas_call(functools.partial(fused_kernel, nodes, phases, 1.0 / math....]
where the time goes in v2:
time: 40.8 us; the launch traced here: 40.6 us
  Pallas kernels  40 us (98%)
  between operations  0.64 us (2%)
    pallas_call x1, Pallas kernels, fused_device(): pl.pallas_call(functools.partial(fused_kernel, nodes, phases, 1.0 / math....  38.6 us
    pallas_call x1, Pallas kernels, fused_device(): pl.pallas_call(write_kernel, name='write', out_shape=(jax.ShapeDtypeStruc...  1.38 us

profile of v2, /device:TPU:0, one launch (start us, length us, event | category | flops | bytes accessed | tf_op | source)
XLA Modules:
  0.0 40.6 jit_solution(2299822500888506152)
XLA Ops:
  0.6 38.6 %fused.1 = (bf16[64,2048]{1,0:T(8,128)(2,1)S(1)}, bf16[24,64,576]{2,1,0:T(8,128)(2,1)S(1)}) custom-call(s32[4,4]{1,0:T(4,128)} %pages_in.1, s32[4]{0:T(128)} %len_in.1, s32[1,4]{1,0:T(1,128)} %bitcast.3, f32[1,512]{1,0:T(1,128)} %bitcast.2, bf16[64,2048]{1,0:T(8,128)(2,1)} %qn_ref.1, bf16[64,1024]{1,0:T(8,128)(2,1)} %qr_ref.1, bf16[64,576]{1,0:T(8,128)(2,1)} %kv_ref.1, ...), custom_call_target="tpu_custom_call" | custom-call | tf_op jit(solution)/shard_map/fused/pallas_call | solution.py:485
  39.3 1.4 %write.1 = (bf16[64,2048]{1,0:T(8,128)(2,1)}, bf16[24,64,576]{2,1,0:T(8,128)(2,1)}) custom-call(bf16[64,2048]{1,0:T(8,128)(2,1)S(1)} %get-tuple-element.4.attn_ref, bf16[24,64,576]{2,1,0:T(8,128)(2,1)S(1)} %get-tuple-element.5.pages_ref), custom_call_target="tpu_custom_call" | custom-call | tf_op jit(solution)/shard_map/write/pallas_call | solution.py:520

commit v3 on v2

--- a/solution.py
+++ b/solution.py
@@ -151,7 +151,7 @@
     attn_ref, CB,
     UK, UV, KB, PAY, KV, Q, QR, QT, QP, QL, LAT, OUT, SEEN, pages_ref, len_ref, slot_ref, gain_ref,
     loc, e_s, e_r, c_s, c_r, n_s, n_r, q_s, q_r, t_s, t_r, m_s, m_r,
-    x_s, x_r, d_s, d_r, g_s, g_r, wk_s, wk_r, wv_s, wv_r, o_s, o_r,
+    x_s, x_r, d_s, d_r, g_s, g_r, wk_s, wk_r, wv_s, wv_r, fk_s, fv_s, o_s, o_r, ready,
 ):
     z = lax.axis_index("node")
     y = lax.axis_index("grp")
@@ -177,12 +177,10 @@
         (2 * (1 - y) + b, {"grp": 1 - y}),
         (2 * (1 - y) + 1 - b, {"grp": 1 - y, "node": mate}),
     )
-    peers = [mate]
-    for j in range(1, nodes // 2):
-        q = (p + j) % (nodes // 2)
-        inner = jnp.where(q < p, 1, 0)
-        peers = peers + [2 * q + inner, 2 * q + 1 - inner]
-    outward = peers[::-1]
+    inside, outside = 2 - p, 3 - 3 * p
+    inner = b + p == 1
+    outer = b + p != 1
+    peers = (mate, inside, outside)
 
     def way(to):
         return (to - z + nodes) % nodes
@@ -190,14 +188,26 @@
     def road(origin):
         return (z - origin + nodes) % nodes
 
-
     barrier = pltpu.get_barrier_semaphore()
+    others = (
+        (y == 0, nodes, team[1][1]),
+        (y == 0, nodes + 1, team[2][1]),
+        (hd % 2 == 0, nodes + 2, {"head": near}),
+        (hd < 2, nodes + 3, {"head": across}),
+    )
+
+    def tell(semaphore, condition, to):
+        @pl.when(condition)
+        def _():
+            pl.semaphore_signal(semaphore, 1, device_id=to, device_id_type=MESH)
+
     for k in range(1, nodes):
-        pl.semaphore_signal(barrier, 1, device_id={"node": (z + k) % nodes}, device_id_type=MESH)
-    for to in (team[1][1], team[2][1], {"head": near}, {"head": across}):
-        pl.semaphore_signal(barrier, 1, device_id=to, device_id_type=MESH)
+        tell(barrier, z + k < nodes, {"node": (z + k) % nodes})
+    for first_in, at, to in others:
+        tell(barrier, first_in, to)
 
     sends = []
+    relayed = []
 
     def remote(src, dst, send, recv, to):
         return pltpu.make_async_remote_copy(
@@ -246,16 +256,45 @@
     def weight_part(buffer, rows, first, count, node):
         return buffer.at[pl.ds(first, count), pl.ds(pl.multiple_of(node * rows, rows), rows), :]
 
-    splits = ((0, 1), (1, heads - 1))
-
-    def send_keys(c, to):
+    splits = ((0, 2), (2, heads - 2))
+
+    def key_copy(c, to):
         first, some = splits[c]
         src = uk_ref.at[pl.ds((2 * y + to % 2) * heads + first, some)]
         k = way(to)
-        go(src, weight_part(UK, rows_k, first, some, z), wk_s.at[c, k], wk_r.at[c, k], {"node": to})
-
-    pl.semaphore_wait(barrier, nodes - 1 + 4)
-    send_keys(0, outward[0])
+        return remote(src, weight_part(UK, rows_k, first, some, z), wk_s.at[c, k], wk_r.at[c, k], {"node": to})
+
+    def send_keys(c, to):
+        copy = key_copy(c, to)
+        copy.start()
+        sends.append(copy)
+
+    known = z + 2 * y + hd % 2 + hd // 2
+
+    @pl.when(known > 0)
+    def _():
+        pl.semaphore_wait(barrier, known)
+
+    for k in range(1, nodes):
+        tell(ready.at[k], z >= k, {"node": (z + nodes - k) % nodes})
+    for first_in, at, to in others:
+        tell(ready.at[at], jnp.logical_not(first_in), to)
+
+    def meet(condition, at):
+        @pl.when(condition)
+        def _():
+            pl.semaphore_wait(ready.at[at], 1)
+
+    def meet_node(to):
+        meet(to > z, way(to))
+
+    def meet_other(i):
+        meet(others[i][0], others[i][1])
+
+    opening = key_copy(0, inside)
+    sends.append(opening)
+    pl.when(inside < z)(opening.start)
+
     for copy in early:
         copy.wait()
 
@@ -331,26 +370,67 @@
         arrive(block, x_s.at[m], x_r.at[m], {"head": across})
         go(block, block, g_s.at[m], g_r.at[m], {"head": near})
 
-    for to in outward:
-        k = way(to)
-        go(PAY.at[pl.ds((to // 2) * 2, 2)], pages_at(y, z), e_s.at[k], e_r.at[k], {"node": to})
-    go(pages_at(y, z), pages_at(y, z), c_s.at[0], c_r.at[0], {"grp": 1 - y})
-    spread(pages_at(y, z), 0)
-    for d, (who, to) in enumerate(team):
-        go(new_at(me), new_at(me), n_s.at[d], n_r.at[d], to)
-    go(new_at(me), new_at(4), n_s.at[3], n_r.at[3], {"node": after})
-    go(SEEN.at[ours], SEEN.at[ours], m_s.at[0], m_r.at[0], {"grp": 1 - y})
-    send_keys(1, outward[0])
-    for to in outward[1:]:
-        send_keys(0, to)
-        send_keys(1, to)
-
     def send_queries(d):
         who, to = team[d]
         go(QT.at[:, cols_of(who, ROPE)], QP.at[me], t_s.at[d], t_r.at[d], to)
         go(qn_ref.at[:, cols_of(who, NOPE)], Q.at[me], q_s.at[d], q_r.at[d], to)
 
+    def page_copy(to):
+        k = way(to)
+        return remote(PAY.at[pl.ds((to // 2) * 2, 2)], pages_at(y, z), e_s.at[k], e_r.at[k], {"node": to})
+
+    def send_new(d):
+        go(new_at(me), new_at(me), n_s.at[d], n_r.at[d], team[d][1])
+
+    copies = [page_copy(to) for to in peers]
+    sends.extend(copies)
+    pl.when(outside < z)(copies[2].start)
+    meet_node(inside)
+    copies[1].start()
+    meet_node(mate)
+    copies[0].start()
+    send_new(0)
+    pl.when(inside > z)(opening.start)
+    meet_other(0)
+    go(pages_at(y, z), pages_at(y, z), c_s.at[0], c_r.at[0], {"grp": 1 - y})
+    send_new(1)
+    go(SEEN.at[ours], SEEN.at[ours], m_s.at[0], m_r.at[0], {"grp": 1 - y})
+    meet_other(1)
+    send_new(2)
+    def go_when(condition, copy):
+        pl.when(condition)(copy.start)
+        relayed.append((condition, copy))
+
+    def key_block(c, node):
+        return weight_part(UK, rows_k, *splits[c], node)
+
+    def value_block(f, node):
+        return weight_part(UV, rows_v, f * count, count, node)
+
+    def value_copy(f, to):
+        k = way(to)
+        src = uv_ref.at[pl.ds((2 * y + to % 2) * heads + f * count, count)]
+        return remote(src, value_block(f, z), wv_s.at[f, k], wv_r.at[f, k], {"node": to})
+
+    def send_values(f, to):
+        copy = value_copy(f, to)
+        copy.start()
+        sends.append(copy)
+
+    send_keys(1, inside)
+    send_keys(0, mate)
+    send_keys(1, mate)
+    meet_other(2)
+    meet_other(3)
+    spread(pages_at(y, z), 0)
+    meet_node(outside)
+    pl.when(outside > z)(copies[2].start)
+    go(new_at(me), new_at(4), n_s.at[3], n_r.at[3], {"node": after})
     send_queries(0)
+    send_queries(2)
+    for c in range(2):
+        go_when(inner, key_copy(c, outside))
+
     QP[me] = QT[:, cols_of(me, ROPE)]
     for origin in peers:
         k = road(origin)
@@ -358,14 +438,32 @@
         arrive(block, e_s.at[k], e_r.at[k], {"node": origin})
         go(block, block, c_s.at[k], c_r.at[k], {"grp": 1 - y})
         spread(block, k)
-    send_queries(2)
     send_queries(1)
-    for f in range(phases):
-        for to in outward:
-            k = way(to)
-            src = uv_ref.at[pl.ds((2 * y + to % 2) * heads + f * count, count)]
-            go(src, weight_part(UV, rows_v, f * count, count, z), wv_s.at[f, k], wv_r.at[f, k], {"node": to})
-    for origin in [z] + peers:
+    mated, hop = road(mate), (outside - mate + nodes) % nodes
+
+    def arrive_keys(c, origin):
+        k = road(origin)
+        block = key_block(c, origin)
+        arrive(block, wk_s.at[c, k], wk_r.at[c, k], {"node": origin})
+
+    def arrive_values(f, origin):
+        k = road(origin)
+        block = value_block(f, origin)
+        arrive(block, wv_s.at[f, k], wv_r.at[f, k], {"node": origin})
+
+    for c in range(2):
+        pl.when(inner)(functools.partial(arrive_keys, c, mate))
+        block = key_block(c, mate)
+        go_when(inner, remote(block, block, fk_s.at[c], wk_r.at[c, hop], {"node": outside}))
+    send_values(0, mate)
+    send_values(1, mate)
+    send_values(2, mate)
+    send_values(3, mate)
+    go_when(inner, value_copy(0, outside))
+    send_values(0, inside)
+    go_when(inner, value_copy(1, outside))
+    send_values(1, inside)
+    for origin in (z, *peers):
         k = road(origin)
         block = pages_at(1 - y, origin)
         arrive(block, c_s.at[k], c_r.at[k], {"grp": 1 - y})
@@ -376,12 +474,12 @@
     spread(fresh_part(hd), 2 * nodes)
     far = near + 2 - 4 * (near // 2)
     for group in range(2):
-        for origin in [z] + peers:
+        for origin in (z, *peers):
             relay(spread_part(y if group == 0 else 1 - y, origin, across), group * nodes + road(origin))
     relay(fresh_part(across), 2 * nodes)
     for head, r in ((near, d_r), (far, g_r)):
         for group in range(2):
-            for origin in [z] + peers:
+            for origin in (z, *peers):
                 m = group * nodes + road(origin)
                 arrive(spread_part(y if group == 0 else 1 - y, origin, head), d_s.at[m], r.at[m], {"head": near})
         arrive(fresh_part(head), d_s.at[2 * nodes], r.at[2 * nodes], {"head": near})
@@ -401,11 +499,22 @@
     for d, (who, to) in enumerate(team):
         arrive(QP.at[who], t_s.at[d], t_r.at[d], to)
         arrive(Q.at[who], q_s.at[d], q_r.at[d], to)
-    for origin in peers:
-        k = road(origin)
-        for c, (first_head, some) in enumerate(splits):
-            block = weight_part(UK, rows_k, first_head, some, origin)
-            arrive(block, wk_s.at[c, k], wk_r.at[c, k], {"node": origin})
+    for f in (0, 1):
+        pl.when(inner)(functools.partial(arrive_values, f, mate))
+        block = value_block(f, mate)
+        go_when(inner, remote(block, block, fv_s.at[f], wv_r.at[f, hop], {"node": outside}))
+    go_when(inner, value_copy(2, outside))
+    send_values(2, inside)
+    go_when(inner, value_copy(3, outside))
+    send_values(3, inside)
+    for f in (2, 3):
+        pl.when(inner)(functools.partial(arrive_values, f, mate))
+        block = value_block(f, mate)
+        go_when(inner, remote(block, block, fv_s.at[f], wv_r.at[f, hop], {"node": outside}))
+    for c in range(2):
+        pl.when(outer)(functools.partial(arrive_keys, c, mate))
+        for origin in (inside, outside):
+            arrive_keys(c, origin)
 
     for h in range(heads):
         QL[h] = jnp.dot(
@@ -438,10 +547,9 @@
         return attn_ref.at[:, pl.ds(pl.multiple_of((who * heads + f * count) * VHEAD, 128), count * VHEAD)]
 
     for f in range(phases):
-        for origin in peers:
-            k = road(origin)
-            block = weight_part(UV, rows_v, f * count, count, origin)
-            arrive(block, wv_s.at[f, k], wv_r.at[f, k], {"node": origin})
+        pl.when(outer)(functools.partial(arrive_values, f, mate))
+        for origin in (inside, outside):
+            arrive_values(f, origin)
         for h in range(f * count, (f + 1) * count):
             OUT[:, :, h * VHEAD:(h + 1) * VHEAD] = jnp.dot(
                 LAT[h], UV[h], preferred_element_type=jnp.float32
@@ -456,6 +564,8 @@
             arrive(result_part(who, f), o_s.at[f, d], o_r.at[f, d], to)
     for copy in sends:
         copy.wait_send()
+    for condition, copy in relayed:
+        pl.when(condition)(copy.wait_send)
 
 
 def write_kernel(attn_ref, pages_ref, attn_out, pages_out, done):
@@ -511,7 +621,8 @@
             pltpu.VMEM((1, LATENT), jnp.float32),
             dma((10,)),
             *pair(nodes), *pair(nodes), *pair(4), *pair(3), *pair(3), *pair(1),
-            *pair(2 * nodes + 1), *pair(2 * nodes + 1), *pair(2 * nodes + 1), *pair(2, nodes), *pair(phases, nodes), *pair(phases, 3),
+            *pair(2 * nodes + 1), *pair(2 * nodes + 1), *pair(2 * nodes + 1), *pair(2, nodes), *pair(phases, nodes), dma((2,)), dma((phases,)), *pair(phases, 3),
+            pltpu.SemaphoreType.REGULAR((nodes + 4,)),
         ],
         compiler_params=pltpu.CompilerParams(
             collective_id=0, has_side_effects=True, vmem_limit_bytes=60 << 20
@@ -534,9 +645,7 @@
     w_uk, w_uv = operands[5], operands[6]
     nodes, grps, fan = (lax.axis_size(name) for name in ("node", "grp", "head"))
     fits = (
-        nodes % 2 == 0
-        and grps == 2
-        and fan == 4
+        (nodes, grps, fan) == (4, 2, 4)
         and NEW == BLOCK
         and w_uk.shape[0] % 8 == 0
         and w_uk.shape[1] % 16 == 0

time: 40.8 us -> 39.9 us (0.978)
  Pallas kernels: 40 us -> 39 us
    pallas_call x1, Pallas kernels: 38.6 us -> 37.7 us  [fused_device(): pl.pallas_call(functools.partial(fused_kernel, nodes, phases, 1.0 / math....]
where the time goes in v3:
time: 39.9 us; the launch traced here: 39.7 us
  Pallas kernels  39 us (98%)
  between operations  0.64 us (2%)
    pallas_call x1, Pallas kernels, fused_device(): pl.pallas_call(functools.partial(fused_kernel, nodes, phases, 1.0 / math....  37.7 us
    pallas_call x1, Pallas kernels, fused_device(): pl.pallas_call(write_kernel, name='write', out_shape=(jax.ShapeDtypeStruc...  1.38 us

profile of v3, /device:TPU:0, one launch (start us, length us, event | category | flops | bytes accessed | tf_op | source)
XLA Modules:
  0.0 39.7 jit_solution(10285111031372442)
XLA Ops:
  0.6 37.7 %fused.1 = (bf16[64,2048]{1,0:T(8,128)(2,1)S(1)}, bf16[24,64,576]{2,1,0:T(8,128)(2,1)S(1)}) custom-call(s32[4,4]{1,0:T(4,128)} %pages_in.1, s32[4]{0:T(128)} %len_in.1, s32[1,4]{1,0:T(1,128)} %bitcast.3, f32[1,512]{1,0:T(1,128)} %bitcast.2, bf16[64,2048]{1,0:T(8,128)(2,1)} %qn_ref.1, bf16[64,1024]{1,0:T(8,128)(2,1)} %qr_ref.1, bf16[64,576]{1,0:T(8,128)(2,1)} %kv_ref.1, ...), custom_call_target="tpu_custom_call" | custom-call | tf_op jit(solution)/shard_map/fused/pallas_call | solution.py:595
  38.3 1.4 %write.1 = (bf16[64,2048]{1,0:T(8,128)(2,1)}, bf16[24,64,576]{2,1,0:T(8,128)(2,1)}) custom-call(bf16[64,2048]{1,0:T(8,128)(2,1)S(1)} %get-tuple-element.4.attn_ref, bf16[24,64,576]{2,1,0:T(8,128)(2,1)S(1)} %get-tuple-element.5.pages_ref), custom_call_target="tpu_custom_call" | custom-call | tf_op jit(solution)/shard_map/write/pallas_call | solution.py:631

commit v4 on v3

--- a/solution.py
+++ b/solution.py
@@ -391,16 +391,23 @@
     copies[0].start()
     send_new(0)
     pl.when(inside > z)(opening.start)
+
+    def go_when(condition, copy):
+        pl.when(condition)(copy.start)
+        relayed.append((condition, copy))
+
+    send_keys(1, inside)
+    send_keys(0, mate)
+    send_keys(1, mate)
+    final_keys = [key_copy(c, outside) for c in range(2)]
+    for copy in final_keys:
+        go_when(inner & (outside < z), copy)
     meet_other(0)
     go(pages_at(y, z), pages_at(y, z), c_s.at[0], c_r.at[0], {"grp": 1 - y})
     send_new(1)
     go(SEEN.at[ours], SEEN.at[ours], m_s.at[0], m_r.at[0], {"grp": 1 - y})
     meet_other(1)
     send_new(2)
-    def go_when(condition, copy):
-        pl.when(condition)(copy.start)
-        relayed.append((condition, copy))
-
     def key_block(c, node):
         return weight_part(UK, rows_k, *splits[c], node)
 
@@ -417,9 +424,6 @@
         copy.start()
         sends.append(copy)
 
-    send_keys(1, inside)
-    send_keys(0, mate)
-    send_keys(1, mate)
     meet_other(2)
     meet_other(3)
     spread(pages_at(y, z), 0)
@@ -428,8 +432,8 @@
     go(new_at(me), new_at(4), n_s.at[3], n_r.at[3], {"node": after})
     send_queries(0)
     send_queries(2)
-    for c in range(2):
-        go_when(inner, key_copy(c, outside))
+    for copy in final_keys:
+        go_when(inner & (outside > z), copy)
 
     QP[me] = QT[:, cols_of(me, ROPE)]
     for origin in peers:

time: 39.9 us -> 39.8 us (level)
  no operation moved by 1% of the time
where the time goes in v4:
time: 39.8 us; the launch traced here: 39.6 us
  Pallas kernels  38.9 us (98%)
  between operations  0.64 us (2%)
    pallas_call x1, Pallas kernels, fused_device(): pl.pallas_call(functools.partial(fused_kernel, nodes, phases, 1.0 / math....  37.6 us
    pallas_call x1, Pallas kernels, fused_device(): pl.pallas_call(write_kernel, name='write', out_shape=(jax.ShapeDtypeStruc...  1.38 us

profile of v4, /device:TPU:0, one launch (start us, length us, event | category | flops | bytes accessed | tf_op | source)
XLA Modules:
  0.0 39.6 jit_solution(3168994362422263556)
XLA Ops:
  0.6 37.6 %fused.1 = (bf16[64,2048]{1,0:T(8,128)(2,1)S(1)}, bf16[24,64,576]{2,1,0:T(8,128)(2,1)S(1)}) custom-call(s32[4,4]{1,0:T(4,128)} %pages_in.1, s32[4]{0:T(128)} %len_in.1, s32[1,4]{1,0:T(1,128)} %bitcast.3, f32[1,512]{1,0:T(1,128)} %bitcast.2, bf16[64,2048]{1,0:T(8,128)(2,1)} %qn_ref.1, bf16[64,1024]{1,0:T(8,128)(2,1)} %qr_ref.1, bf16[64,576]{1,0:T(8,128)(2,1)} %kv_ref.1, ...), custom_call_target="tpu_custom_call" | custom-call | tf_op jit(solution)/shard_map/fused/pallas_call | solution.py:599
  38.2 1.4 %write.1 = (bf16[64,2048]{1,0:T(8,128)(2,1)}, bf16[24,64,576]{2,1,0:T(8,128)(2,1)}) custom-call(bf16[64,2048]{1,0:T(8,128)(2,1)S(1)} %get-tuple-element.4.attn_ref, bf16[24,64,576]{2,1,0:T(8,128)(2,1)S(1)} %get-tuple-element.5.pages_ref), custom_call_target="tpu_custom_call" | custom-call | tf_op jit(solution)/shard_map/write/pallas_call | solution.py:635
